TPU v7x, 32 devices: a whole 2x2x4 slice. The times are simulated.
32 devices in a mesh: row: 4 (over z), col: 8 (over y, x, core).
Axes of the slice: x: 2, y: 2, z: 4, core: 2. Of those that a mesh axis runs over, the one named last changes fastest.
Arguments:
- points_rhs: bfloat16 [262144, 16], P(('row', 'col')), may hold values from -6 to 6
- leaf_basis: bfloat16 [1024, 256, 64], P(('row', 'col')), may hold values from -0.375 to 0.375
- near_src: int32 [1024, 2], P(('row', 'col')), may hold values from -1 to 1023, as said below
- near_blocks: bfloat16 [1024, 2, 256, 256], P(('row', 'col')), may hold values from -0.25 to 0.25
- transfer_first: bfloat16 [1024, 64, 64], P(('row', 'col')), may hold values from -0.5 to 0.5
- transfer_second: bfloat16 [512, 64, 64], P(('row', 'col')), may hold values from -0.5 to 0.5
- transfer_third: bfloat16 [256, 64, 64], P(('row', 'col')), may hold values from -0.5 to 0.5
- far_zero: int32 [1024, 8], P(('row', 'col')), may hold values from -1 to 1023, as said below
- far_one: int32 [512, 8], P(('row', 'col')), may hold values from -1 to 511, as said below
- far_two: int32 [256, 8], P(('row', 'col')), may hold values from -1 to 255, as said below
- far_three: int32 [128, 8], P(('row', 'col')), may hold values from -1 to 127, as said below
- couple_zero: bfloat16 [1024, 8, 64, 64], P(('row', 'col')), may hold values from -0.25 to 0.25
- couple_one: bfloat16 [512, 8, 64, 64], P(('row', 'col')), may hold values from -0.25 to 0.25
- couple_two: bfloat16 [256, 8, 64, 64], P(('row', 'col')), may hold values from -0.25 to 0.25
- couple_three: bfloat16 [128, 8, 64, 64], P(('row', 'col')), may hold values from -0.25 to 0.25
Outputs:
- product: bfloat16 [262144, 16], P(('row', 'col'))
Inputs may be any that keep to these rules, and one draw needn't show every extreme that they name: `near_src`: each entry is -1 or a leaf whose index differs from its row's by at most 2; -1 only where that leaf would lie outside the grid. `far_zero`: each row has 7 or 8 live entries, first in the row; a live entry of leaf i lies in the same aligned block of 256 leaves as i. `far_one`: each row has 7 or 8 live entries, first in the row; a live entry of cluster i lies in the same aligned block of 128 clusters as i. `far_two`: each row has 7 or 8 live entries, first in the row; a live entry of cluster i lies in the same aligned block of 64 clusters as i. `far_three`: each row has 7 or 8 live entries, first in the row; live entries may name any cluster of the level.
All inputs are finite; a program needn't handle non-finite values.
Results may differ from a plain program's by a relative error of at most 0.0044.
Values may be sent and summed in bfloat16 or wider, within the bound.
No kernel may reach another device: no remote copies, remote signals or barrier semaphores. Data moves between devices by JAX's collectives and lax.ppermute only.
A program may use at most 128 MiB of HBM per device.

v0:
```python
import functools

import jax
import jax.numpy as jnp
from jax import lax
from jax.experimental import pallas as pl
from jax.experimental.pallas import tpu as pltpu
from jax.sharding import PartitionSpec as P


SLOTS = 8
HALO = 2
STEPS = 8
CHUNKS = 4
SENDS = 2


NT = (((1,), (1,)), ((), ()))
NN = (((1,), (0,)), ((), ()))
TN = (((0,), (0,)), ((), ()))

VMEM = pl.BlockSpec(memory_space=pltpu.VMEM)
SMEM = pl.BlockSpec(memory_space=pltpu.SMEM)
HBM = pl.BlockSpec(memory_space=pltpu.HBM)
ANY = pl.BlockSpec(memory_space=pl.ANY)


def in_hbm(v):
    return pltpu.with_memory_space_constraint(v, pltpu.HBM)


def dot(a, b, dims):
    return lax.dot_general(a, b, dims, preferred_element_type=jnp.float32)


def low_half(shape):
    return lax.broadcasted_iota(jnp.int32, shape, len(shape) - 1) < shape[-1] // 2


def copies(pairs, sems):
    return [pltpu.make_async_copy(src, dst, sems.at[i]) for i, (src, dst) in enumerate(pairs)]


def edge_blocks(ref, x_ref, at, width, first):
    for b in range(width // 128):
        ref[first + b] = x_ref[:, at + b * 128 : at + (b + 1) * 128]


def upward_kernel(
    n0, leaf, x_hbm, basis_hbm, e1_hbm, e2_hbm, e3_hbm, skel_ref, near_row_ref, far_row_ref, chip_ref, core_ref,
    x_ref, basis_ref, e1_ref, e2_ref, e3_ref, sems, basis_sems,
):
    chunk = n0 // 2 // CHUNKS
    top = n0 // 16
    width = HALO * leaf
    fetch = copies([(x_hbm, x_ref), (e1_hbm, e1_ref), (e2_hbm, e2_ref), (e3_hbm, e3_ref)], sems)
    spans = [pl.ds(c * chunk, chunk) for c in range(CHUNKS)]
    fetch_basis = copies([(basis_hbm.at[s], basis_ref.at[s]) for s in spans], basis_sems)
    fetch[0].start()
    for c in fetch_basis:
        c.start()
    for c in fetch[1:]:
        c.start()
    fetch[0].wait()

    def edges(even, head_to, tail_to):
        @pl.when(even)
        def _():
            edge_blocks(head_to[0], x_ref, 0, width, head_to[1])
            edge_blocks(tail_to[0], x_ref, n0 * leaf - width, width, tail_to[1])

        @pl.when(jnp.logical_not(even))
        def _():
            edge_blocks(tail_to[0], x_ref, 0, width, tail_to[1])
            edge_blocks(head_to[0], x_ref, n0 * leaf - width, width, head_to[1])

    edges(lax.axis_index("row") % 2 == 0, (far_row_ref, top), (near_row_ref, top))
    edges(lax.axis_index("col") % 2 == 0, (chip_ref, 0), (core_ref, 0))
    nrhs = x_ref.shape[0]
    low = low_half((nrhs, 128))
    level = []
    for p in range(n0 // 2):
        if p % chunk == 0:
            fetch_basis[p // chunk].wait()
        xs = jnp.concatenate([x_ref[:, (2 * p + h) * leaf : (2 * p + h + 1) * leaf] for h in range(2)], axis=0)
        both = dot(xs, basis_ref[p], NT)
        level.append(jnp.where(low, both[:nrhs], both[nrhs:]).astype(jnp.bfloat16))
        skel_ref[p] = level[p]
    base = n0 // 2
    for step, e_ref in enumerate((e1_ref, e2_ref, e3_ref)):
        fetch[1 + step].wait()
        parents = [dot(v, e_ref[p], NN) for p, v in enumerate(level)]
        level = [
            jnp.concatenate([parents[2 * q], parents[2 * q + 1]], axis=1).astype(jnp.bfloat16)
            for q in range(len(parents) // 2)
        ]
        for q, v in enumerate(level):
            if step < 2:
                skel_ref[base + q] = v
            else:
                near_row_ref[q] = v
                far_row_ref[q] = v
        base += len(level)


def pack_kernel(rows, cols, top, skel_ref, chip_ref, after_ref, own_ref, *refs):
    del after_ref
    own, width = skel_ref.shape[0], chip_ref.shape[0]
    tops, mine_ref = (own_ref, *reversed(refs[: rows - 1])), refs[rows - 1]
    mine_ref[:own] = skel_ref[...]
    for k in range(rows):
        mine_ref[own + k * top : own + (k + 1) * top] = tops[k][:top]
    base = own + rows * top
    mine_ref[base : base + width] = chip_ref[...]
    row, col = lax.axis_index("row"), lax.axis_index("col")
    odd = row % 2
    from_near = (col == cols - 1) == (odd == 1)
    partner = jnp.where(from_near, 1, row ^ (row + 2 * odd - 1))
    for m in range(1, rows.bit_length()):
        k = 2**m - 1
        if k >= rows:
            break

        @pl.when((partner == k) | (k == 1))
        def _(k=k):
            mine_ref[base + width :] = tops[k][top:]


def side_by_side(s_ref, i, c_ref, at):
    for q in range(SLOTS // 2):
        c_ref[at, :, q * 128 : (q + 1) * 128] = jnp.concatenate([s_ref[i, 2 * q], s_ref[i, 2 * q + 1]], axis=1)


def fold_kernel(
    n0, cols, rows, f0_hbm, f1_hbm, f2_hbm, f3_hbm, s1_hbm, s2_hbm, s3_hbm,
    i0_ref, i1_ref, i2_ref, i3_ref, c_ref, f0_ref, f1_ref, f2_ref, f3_ref, s1_ref, s2_ref, s3_ref, sems, block_sems,
):
    row, col = lax.axis_index("row"), lax.axis_index("col")
    pairs = (n0 // 2 + n0 // 4 + n0 // 8) + rows * (n0 // 16)
    lists = copies([(f0_hbm, f0_ref), (f1_hbm, f1_ref), (f2_hbm, f2_ref), (f3_hbm, f3_ref)], sems)
    n3 = n0 // 8
    streams = ((s3_hbm, s3_ref), (s2_hbm, s2_ref), (s1_hbm, s1_ref))

    def chunk(step):
        out = []
        for n, (src, dst) in enumerate(streams):
            size = src.shape[0] // CHUNKS
            span = pl.ds(step * size, size)
            out.append(pltpu.make_async_copy(src.at[span], dst.at[span], block_sems.at[step, n]))
        return out

    for c in lists:
        c.start()
    for step in range(CHUNKS):
        for c in chunk(step):
            c.start()
    for c in lists:
        c.wait()

    def place(f, slot_axis, per, first_pair, kz):
        dev = f // per
        pos = f % per
        k = (dev % cols) ^ col
        if kz:
            first_pair = first_pair + ((dev // cols) ^ row) * (per // 2)
        block = (k % 2) * (cols // 2) + k // 2
        spot = (block * pairs + first_pair) * 2 + pos
        slot = lax.broadcasted_iota(jnp.int32, f.shape, slot_axis)
        spot = spot ^ (slot % 2)
        return jnp.where(f >= 0, spot, cols * pairs * 2)

    i0_ref[...] = place(f0_ref[...], 0, n0, 0, False)
    i1_ref[...] = place(f1_ref[...], 0, n0 // 2, n0 // 2, False)
    i2_ref[...] = place(f2_ref[...], 1, n0 // 4, n0 // 2 + n0 // 4, False)
    i3_ref[...] = place(f3_ref[...], 1, n0 // 8, n0 // 2 + n0 // 4 + n0 // 8, True)

    @pl.loop(0, CHUNKS)
    def _(step):
        for c in chunk(step):
            c.wait()
        for s_ref, first in ((s3_ref, 0), (s2_ref, n3), (s1_ref, 3 * n3)):
            count = s_ref.shape[0] // CHUNKS
            for j in range(count):
                side_by_side(s_ref, step * count + j, c_ref, first + step * count + j)


def near_kernel(
    n0, leaf, cols, near_src_hbm, x_hbm, blocks_hbm, s_hbm, after_ref, near_ref, c_ref,
    x_ref, near_src_ref, blocks_ref, s_ref, sems, block_sems,
):
    del after_ref
    small = copies([(near_src_hbm, near_src_ref), (x_hbm, x_ref.at[:, pl.ds(0, n0 * leaf)])], sems)

    streams = ((blocks_hbm, blocks_ref), (s_hbm, s_ref))

    def chunk(step):
        span = pl.ds(step * (n0 // STEPS), n0 // STEPS)
        return copies([(src.at[span], dst.at[span]) for src, dst in streams], block_sems.at[step])

    for c in small:
        c.start()
    for step in range(STEPS):
        for c in chunk(step):
            c.start()
    x_ref[:, n0 * leaf :] = jnp.zeros((x_ref.shape[0], leaf), jnp.bfloat16)
    for c in small:
        c.wait()
    first_leaf = (lax.axis_index("row") * cols + lax.axis_index("col")) * n0

    @pl.loop(0, STEPS)
    def _(step):
        for c in chunk(step):
            c.wait()
        for j in range(n0 // STEPS):
            i = step * (n0 // STEPS) + j
            side_by_side(s_ref, i, c_ref, i)
            acc = None
            for s in range(2):
                at = near_src_ref[s, i] - first_leaf
                at = jnp.where((at >= 0) & (at < n0), at, n0)
                xs = x_ref[:, pl.ds(pl.multiple_of(at * leaf, leaf), leaf)]
                part = dot(xs, blocks_ref[i, s], NT)
                acc = part if acc is None else acc + part
            near_ref[:, pl.ds(pl.multiple_of(i * leaf, leaf), leaf)] = acc


def join_kernel(parts, core_ref, after_ref, *refs):
    del after_ref
    out_ref = refs[parts]
    size = refs[0].shape[0]
    for j in range(parts):
        out_ref[j * size : (j + 1) * size] = refs[j][...]
    out_ref[parts * size :] = core_ref[...]


def product_kernel(
    n0, leaf, cols, pairs, i0_hbm, i1_hbm, i2_hbm, i3_hbm, near_src_hbm, a_ref, b_ref, c_ref, c0_ref,
    e1_hbm, e2_hbm, e3_hbm, basis_ref, near_in_ref, x_hbm, blocks_hbm, out_hbm, near_ref,
    i0_ref, i1_ref, i2_ref, i3_ref, near_src_ref, table_ref, field_ref, down_ref, e_ref, x_ref, blocks_ref, out_ref,
    list_sems, sems, out_sems,
):
    del near_in_ref
    nrhs = out_ref.shape[0]
    low = low_half((nrhs, 128))
    chips = cols // 2
    width = HALO * leaf // 128
    block = pairs + 2 * width
    side = 2 * HALO * leaf
    n1, n2, n3 = n0 // 2, n0 // 4, n0 // 8
    ends = [pl.ds(0, HALO), pl.ds(n0 - HALO, HALO)]
    lists = copies(
        [
            (i0_hbm, i0_ref), (i1_hbm, i1_ref), (i2_hbm, i2_ref), (i3_hbm, i3_ref), (near_src_hbm, near_src_ref),
        ],
        list_sems,
    )
    fetch = copies(
        [
            (x_hbm.at[:, pl.ds(0, side)], x_ref.at[:, pl.ds(HALO * leaf, side)]),
            (x_hbm.at[:, pl.ds(n0 * leaf - side, side)], x_ref.at[:, pl.ds(HALO * leaf + side, side)]),
            (blocks_hbm.at[ends[0]], blocks_ref.at[pl.ds(0, HALO)]),
            (blocks_hbm.at[ends[1]], blocks_ref.at[pl.ds(HALO, HALO)]),
            (e3_hbm, e_ref.at[pl.ds(0, n3)]),
            (e2_hbm, e_ref.at[pl.ds(n3, n2)]),
            (e1_hbm, e_ref.at[pl.ds(n3 + n2, n1)]),
        ],
        sems,
    )
    for f in lists + fetch:
        f.start()

    parts = 1
    wide = pairs // parts

    @pl.loop(0, chips * parts)
    def _(t):
        chip, part = t // parts, t % parts
        for h, ref in enumerate((a_ref, b_ref)):
            for j in range(wide):
                v = ref[chip * block + part * wide + j]
                at = ((h * chips + chip) * pairs + part * wide + j) * 2
                table_ref[at] = v
                table_ref[at + 1] = jnp.concatenate([v[:, 64:], v[:, :64]], axis=1)

    table_ref[2 * cols * pairs] = jnp.zeros((nrhs, 128), jnp.bfloat16)
    table_ref[2 * cols * pairs + 1] = jnp.zeros((nrhs, 128), jnp.bfloat16)
    for f in lists:
        f.wait()

    @pl.loop(0, n3)
    def _(t):
        for per, first, spot in (
            (1, 0, lambda k, i: i3_ref[i, k]),
            (2, n3, lambda k, i: i2_ref[i, k]),
            (4, n3 + n2, lambda k, i: i1_ref[k, i]),
            (8, n3 + n2 + n1, lambda k, i: i0_ref[k, i]),
        ):
            for j in range(per):
                i = t * per + j
                xs = [
                    jnp.where(low, table_ref[spot(2 * q, i)], table_ref[spot(2 * q + 1, i)])
                    for q in range(SLOTS // 2)
                ]
                blocks = c_ref[first + i] if per < 8 else c0_ref[i]
                field_ref[first + i] = dot(blocks, jnp.concatenate(xs, axis=1), NT)

    row, col = lax.axis_index("row"), lax.axis_index("col")
    odd = col % 2
    across = col + 2 * odd - 1
    inside = (across >= 0) & (across < cols)
    chip = jnp.where(inside, (col ^ across) // 2, chips - 1)
    at_edge = chip * block + pairs + jnp.where(inside, 0, width)
    at_core = chips * block
    left = jnp.where(odd == 1, at_core, at_edge)
    right = jnp.where(odd == 1, at_edge, at_core)
    end = HALO * leaf + 2 * side
    for j in range(width):
        x_ref[:, j * 128 : (j + 1) * 128] = b_ref[left + j]
        x_ref[:, end + j * 128 : end + (j + 1) * 128] = b_ref[right + j]
    zero = 6 * HALO
    x_ref[:, zero * leaf :] = jnp.zeros((nrhs, leaf), jnp.bfloat16)
    for f in fetch:
        f.wait()
    first_leaf = (row * cols + col) * n0

    for j in range(HALO):
        for b, i, shift in ((j, j, HALO), (HALO + j, n0 - HALO + j, 5 * HALO - n0)):
            acc = None
            for s in range(2):
                src = near_src_ref[s, i]
                at = jnp.where(src >= 0, src - first_leaf + shift, zero)
                xs = x_ref[:, pl.ds(pl.multiple_of(at * leaf, leaf), leaf)]
                part = dot(xs, blocks_ref[b, s], NT)
                acc = part if acc is None else acc + part
            near_ref[:, pl.ds(pl.multiple_of(i * leaf, leaf), leaf)] = acc

    down = [field_ref[p].astype(jnp.bfloat16) for p in range(n3)]
    for p in range(7 * n3):
        pair = dot(e_ref[p], down[p], NN)
        for h in range(2):
            c = n3 + 2 * p + h
            down.append((field_ref[c] + pair[h * 64 : (h + 1) * 64]).astype(jnp.bfloat16))
    for i in range(n0):
        down_ref[i] = down[7 * n3 + i]

    def send(t):
        span = pl.ds(pl.multiple_of(t * n0 // SENDS * leaf, leaf), n0 // SENDS * leaf)
        return pltpu.make_async_copy(out_ref.at[:, span], out_hbm.at[:, span], out_sems.at[t])

    @pl.loop(0, SENDS)
    def _(t):
        for j in range(n0 // SENDS):
            i = t * (n0 // SENDS) + j
            d = down_ref[i]
            far = dot(d, basis_ref[t * (n1 // SENDS) + j // 2, (j % 2) * 64 : (j % 2 + 1) * 64], TN)
            at = pl.ds(pl.multiple_of(i * leaf, leaf), leaf)
            out_ref[:, at] = (far + near_ref[:, at]).astype(jnp.bfloat16)
        send(t).start()

    for t in range(SENDS):
        send(t).wait()


def shards(
    points_rhs, leaf_basis, near_src, near_blocks, transfer_first, transfer_second, transfer_third,
    far_zero, far_one, far_two, far_three, couple_zero, couple_one, couple_two, couple_three,
):
    bf, f32, i32 = jnp.bfloat16, jnp.float32, jnp.int32
    n0, leaf, rank = leaf_basis.shape
    nrhs = points_rhs.shape[1]
    rows, cols = lax.axis_size("row"), lax.axis_size("col")
    n1, n2, n3 = n0 // 2, n0 // 4, n0 // 8
    x = points_rhs.T
    basis = leaf_basis.transpose(0, 2, 1).reshape(n1, 2 * rank, leaf)
    e1, e2, e3 = (
        e.reshape(e.shape[0] // 2, 2 * rank, rank) for e in (transfer_first, transfer_second, transfer_third)
    )
    own_pairs = (n0 + n1 + n2) // 2
    top_pairs = n3 // 2
    width = HALO * leaf // 128
    pairs = own_pairs + rows * top_pairs

    def blocks_of(n):
        return jax.ShapeDtypeStruct((n, nrhs, 2 * rank), bf)

    def params(mib):
        return pltpu.CompilerParams(vmem_limit_bytes=mib << 20)

    def cost(us):
        return pl.CostEstimate(flops=int(us * 2e8), bytes_accessed=int(us * 3e6), transcendentals=0)

    skel, near_row, far_row, chip, core = pl.pallas_call(
        functools.partial(upward_kernel, n0, leaf),
        out_shape=[blocks_of(own_pairs), blocks_of(top_pairs + width), blocks_of(top_pairs + width)]
        + [blocks_of(width)] * 2,
        in_specs=[HBM] * 5,
        out_specs=[VMEM] * 5,
        scratch_shapes=[pltpu.VMEM(v.shape, bf) for v in (x, basis, e1, e2, e3)]
        + [pltpu.SemaphoreType.DMA((4,)), pltpu.SemaphoreType.DMA((CHUNKS,))],
        compiler_params=params(12),
        cost_estimate=cost(2),
        name="upward",
    )(*map(in_hbm, (x, basis, e1, e2, e3)))

    def swap(v, axis, size, k):
        return lax.ppermute(v, axis, [(i, i ^ k) for i in range(size)])

    tops = [None] * rows
    for k in reversed(range(1, rows)):
        mersenne = (k & (k + 1)) == 0
        sent = near_row if k == 1 else far_row if mersenne else near_row[:top_pairs]
        tops[k] = swap(sent, "row", rows, k)

    lists = (far_zero.T, far_one.T, far_two, far_three)
    blocks = (couple_one, couple_two, couple_three)
    i0, i1, i2, i3, c = pl.pallas_call(
        functools.partial(fold_kernel, n0, cols, rows),
        out_shape=[jax.ShapeDtypeStruct(f.shape, i32) for f in lists]
        + [jax.ShapeDtypeStruct((7 * n3, rank, SLOTS * rank), bf)],
        in_specs=[HBM] * 7,
        out_specs=[VMEM] * 5,
        scratch_shapes=[pltpu.VMEM(f.shape, i32) for f in lists]
        + [pltpu.VMEM(s.shape, bf) for s in blocks]
        + [pltpu.SemaphoreType.DMA((4,)), pltpu.SemaphoreType.DMA((CHUNKS, 3))],
        compiler_params=params(14),
        cost_estimate=cost(4),
        name="fold",
    )(*map(in_hbm, (*lists, *blocks)))

    mine = pl.pallas_call(
        functools.partial(pack_kernel, rows, cols, top_pairs),
        out_shape=blocks_of(pairs + 2 * width),
        in_specs=[VMEM, VMEM, ANY] + [VMEM] * rows,
        out_specs=VMEM,
        compiler_params=params(4),
        name="pack",
    )(skel, chip, i3, near_row, *reversed(tops[1:]))

    parts = [None] * (cols // 2)
    parts[0] = mine
    for k in reversed(range(1, cols // 2)):
        parts[k] = swap(mine, "col", cols, 2 * k)

    near, c0 = pl.pallas_call(
        functools.partial(near_kernel, n0, leaf, cols),
        out_shape=[
            jax.ShapeDtypeStruct((nrhs, n0 * leaf), f32),
            jax.ShapeDtypeStruct((n0, rank, SLOTS * rank), bf),
        ],
        in_specs=[HBM] * 4 + [ANY],
        out_specs=[VMEM] * 2,
        scratch_shapes=[
            pltpu.VMEM((nrhs, (n0 + 1) * leaf), bf),
            pltpu.SMEM((2, n0), i32),
            pltpu.VMEM(near_blocks.shape, bf),
            pltpu.VMEM(couple_zero.shape, bf),
            pltpu.SemaphoreType.DMA((2,)),
            pltpu.SemaphoreType.DMA((STEPS, 2)),
        ],
        compiler_params=params(18),
        cost_estimate=cost(6),
        name="near",
    )(*map(in_hbm, (near_src.T, x, near_blocks, couple_zero)), mine)

    ours = pl.pallas_call(
        functools.partial(join_kernel, cols // 2),
        out_shape=blocks_of(cols // 2 * mine.shape[0] + width),
        in_specs=[VMEM, ANY] + [VMEM] * (cols // 2),
        out_specs=VMEM,
        compiler_params=params(8),
        name="join",
    )(core, near, *parts)
    theirs = swap(ours, "col", cols, 1)

    out, _ = pl.pallas_call(
        functools.partial(product_kernel, n0, leaf, cols, pairs),
        out_shape=[jax.ShapeDtypeStruct((nrhs, n0 * leaf), bf), jax.ShapeDtypeStruct((nrhs, n0 * leaf), f32)],
        in_specs=[ANY] * 4 + [HBM] + [VMEM] * 4 + [HBM] * 3 + [VMEM] * 2 + [HBM] * 2,
        out_specs=[HBM, VMEM],
        input_output_aliases={13: 1},
        scratch_shapes=[pltpu.SMEM(v.shape, i32) for v in (i0, i1, i2, i3, near_src.T)]
        + [
            pltpu.VMEM((2 * cols * pairs + 2, nrhs, 2 * rank), bf),
            pltpu.VMEM((15 * n3, rank, nrhs), f32),
            pltpu.VMEM((n0, rank, nrhs), bf),
            pltpu.VMEM((7 * n3, 2 * rank, rank), bf),
            pltpu.VMEM((nrhs, (6 * HALO + 1) * leaf), bf),
            pltpu.VMEM((2 * HALO, *near_blocks.shape[1:]), bf),
            pltpu.VMEM((nrhs, n0 * leaf), bf),
            pltpu.SemaphoreType.DMA((5,)),
            pltpu.SemaphoreType.DMA((7,)),
            pltpu.SemaphoreType.DMA((SENDS,)),
        ],
        compiler_params=params(28),
        cost_estimate=cost(5),
        name="product",
    )(
        i0, i1, i2, i3, in_hbm(near_src.T), ours, theirs, c, c0, *map(in_hbm, (e1, e2, e3)), basis, near,
        *map(in_hbm, (x, near_blocks)),
    )
    return out.T


def solution(mesh):
    whole = P(("row", "col"))
    return jax.shard_map(
        shards,
        mesh=mesh,
        in_specs=(whole,) * 15,
        out_specs=whole,
        check_vma=False,
    )
```

profile of v0, /device:TPU:0, one launch (start us, length us, event | category | flops | bytes accessed | tf_op | source)
XLA Modules:
  0.0 32.3 jit_solution(10905960624430929757)
XLA Ops:
  0.0 2.7 %upward.1 = (bf16[28,16,128]{2,1,0:T(8,128)(2,1)S(1)}, bf16[6,16,128]{2,1,0:T(8,128)(2,1)S(1)}, bf16[6,16,128]{2,1,0:T(8,128)(2,1)S(1)}, bf16[4,16,128]{2,1,0:T(8,128)(2,1)S(1)}, bf16[4,16,128]{2,1,0:T(8,128)(2,1)S(1)}) custom-call(bf16[16,8192]{1,0:T(8,128)(2,1)} %bitcast.13, bf16[16,128,256]{2,1,0:T(8,128)(2,1)} %bitcast.11, ...), custom_call_target="tpu_custom_call" | custom-call | flops 400000000 | bytes 6000000 | tf_op jit(solution)/shard_map/upward/pallas_call | solution.py:392
  2.7 3.1 %collective-permute-start.2 = (bf16[6,16,128]{2,1,0:T(8,128)(2,1)S(1)}, bf16[6,16,128]{2,1,0:T(8,128)(2,1)S(1)}, u32[]{:S(2)}, u32[]{:S(2)}) collective-permute-start(bf16[6,16,128]{2,1,0:T(8,128)(2,1)S(1)} %get-tuple-element.25.own_ref), channel_id=1, source_target_pairs={{0,8},{8,0},{16,24},{24,16},{1,9},{9,1},{17,25},{25,17},{2,10},{10... | collective-permute-start | bytes 73736 | tf_op jit(solution)/shard_map/ppermute | solution.py:406
  5.8 2.6 %collective-permute-start.1 = (bf16[2,16,128]{2,1,0:T(8,128)(2,1)S(1)}, bf16[2,16,128]{2,1,0:T(8,128)(2,1)S(1)}, u32[]{:S(2)}, u32[]{:S(2)}) collective-permute-start(bf16[2,16,128]{2,1,0:T(8,128)(2,1)S(1)} %slice.3), channel_id=1, source_target_pairs={{0,16},{8,24},{16,0},{24,8},{1,17},{9,25},{17,1},{25,9},{2,18},{10... | collective-permute-start | bytes 24584 | tf_op jit(solution)/shard_map/ppermute | solution.py:406
  8.4 0.0 collective-permute-start
  8.4 2.6 %fold.1 = (s32[8,32]{1,0:T(8,128)S(1)}, s32[8,16]{1,0:T(8,128)S(1)}, s32[8,8]{1,0:T(8,128)S(1)}, s32[4,8]{1,0:T(4,128)S(1)}, bf16[28,64,512]{2,1,0:T(8,128)(2,1)S(1)}) custom-call(s32[8,32]{1,0:T(8,128)} %bitcast.24, s32[8,16]{1,0:T(8,128)} %bitcast.25, s32[8,8]{1,0:T(8,128)} %f2_hbm.1, s32[4,8]{1,0:T(4,128)} %f3_hbm.1, bf16[16,8,64,64]{3,2,1,0:T(8,128)(2,1)} %s1_hbm.1, ...), custom_call_target="tpu_custom_call" | custom-call | flops 800000000 | bytes 12000000 | tf_op jit(solution)/shard_map/fold/pallas_call | solution.py:416
  11.0 0.0 collective-permute-done.1.refs_1_
  11.0 3.0 %collective-permute-done.refs_0_ = bf16[6,16,128]{2,1,0:T(8,128)(2,1)S(1)} collective-permute-done((bf16[6,16,128]{2,1,0:T(8,128)(2,1)S(1)}, bf16[6,16,128]{2,1,0:T(8,128)(2,1)S(1)}, u32[]{:S(2)}, u32[]{:S(2)}) %collective-permute-start) | collective-permute-done | bytes 24608 | tf_op jit(solution)/shard_map/ppermute | solution.py:406
  14.0 0.0 collective-permute-done.2.refs_2_
  14.1 2.5 %collective-permute-start.5 = (bf16[44,16,128]{2,1,0:T(8,128)(2,1)S(1)}, bf16[44,16,128]{2,1,0:T(8,128)(2,1)S(1)}, u32[]{:S(2)}, u32[]{:S(2)}) collective-permute-start(bf16[44,16,128]{2,1,0:T(8,128)(2,1)S(1)} %pack.1.after_ref.refs_0_), channel_id=1, source_target_pairs={{0,6},{1,7},{2,4},{3,5},{4,2},{5,3},{6,0},{7,1},{8,14},{9,15},{10,... | collective-permute-start | bytes 540680 | tf_op jit(solution)/shard_map/ppermute | solution.py:406
  16.6 0.5 %collective-permute-start.4 = (bf16[44,16,128]{2,1,0:T(8,128)(2,1)S(1)}, bf16[44,16,128]{2,1,0:T(8,128)(2,1)S(1)}, u32[]{:S(2)}, u32[]{:S(2)}) collective-permute-start(bf16[44,16,128]{2,1,0:T(8,128)(2,1)S(1)} %pack.1.after_ref.refs_0_), channel_id=1, source_target_pairs={{0,4},{1,5},{2,6},{3,7},{4,0},{5,1},{6,2},{7,3},{8,12},{9,13},{10,... | collective-permute-start | bytes 540680 | tf_op jit(solution)/shard_map/ppermute | solution.py:406
  17.1 0.5 %collective-permute-start.3 = (bf16[44,16,128]{2,1,0:T(8,128)(2,1)S(1)}, bf16[44,16,128]{2,1,0:T(8,128)(2,1)S(1)}, u32[]{:S(2)}, u32[]{:S(2)}) collective-permute-start(bf16[44,16,128]{2,1,0:T(8,128)(2,1)S(1)} %pack.1.after_ref.refs_0_), channel_id=1, source_target_pairs={{0,2},{1,3},{2,0},{3,1},{4,6},{5,7},{6,4},{7,5},{8,10},{9,11},{10,... | collective-permute-start | bytes 540680 | tf_op jit(solution)/shard_map/ppermute | solution.py:406
  17.6 7.5 %near.1 = (f32[16,8192]{1,0:T(8,128)S(1)}, bf16[32,64,512]{2,1,0:T(8,128)(2,1)S(1)}) custom-call(s32[2,32]{1,0:T(2,128)} %bitcast.22, bf16[16,8192]{1,0:T(8,128)(2,1)} %bitcast.14, bf16[32,2,256,256]{3,2,1,0:T(8,128)(2,1)} %blocks_hbm.3, bf16[32,8,64,64]{3,2,1,0:T(8,128)(2,1)} %s_hbm.1, bf16[44,16,128]{2,1,0:T(8,128)(2,1)S(1)} %pack.1.after_ref.refs_0_), custom_call_target="tpu_custom_call" | custom-call | flops 1200000000 | bytes 18000000 | tf_op jit(solution)/shard_map/near/pallas_call | solution.py:444
  25.1 0.0 copy-start
  25.1 0.0 collective-permute-done.5.refs_3_
  25.1 0.0 collective-permute-done.4.refs_2_
  25.1 0.0 collective-permute-done.3.refs_1_
  25.1 0.1 join.1.a_ref
  25.2 0.1 collective-permute-start.6
  25.3 2.2 %collective-permute-done.6.b_ref = bf16[180,16,128]{2,1,0:T(8,128)(2,1)S(1)} collective-permute-done((bf16[180,16,128]{2,1,0:T(8,128)(2,1)S(1)}, bf16[180,16,128]{2,1,0:T(8,128)(2,1)S(1)}, u32[]{:S(2)}, u32[]{:S(2)}) %collective-permute-start.6) | collective-permute-done | bytes 737312 | tf_op jit(solution)/shard_map/ppermute | solution.py:406
  27.5 0.0 copy-done
  27.5 4.8 %product.1 = (bf16[16,8192]{1,0:T(8,128)(2,1)}, f32[16,8192]{1,0:T(8,128)S(1)}) custom-call(s32[8,32]{1,0:T(8,128)S(1)} %get-tuple-element.18.i0_hbm, s32[8,16]{1,0:T(8,128)S(1)} %get-tuple-element.19.i1_hbm, s32[8,8]{1,0:T(8,128)S(1)} %get-tuple-element.20.i2_hbm, s32[4,8]{1,0:T(4,128)S(1)} %get-tuple-element.21.after_ref.i3_hbm, ...), custom_call_target="tpu_custom_call", output_to_operand_aliasing={{1}: (13, {})} | custom-call | flops 1000000000 | bytes 15000000 | tf_op jit(solution)/shard_map/product/pallas_call | solution.py:475
  (2 shorter events, 0.0 us)
Async XLA Ops:
  2.7 11.3 %collective-permute-start.2 = (bf16[6,16,128]{2,1,0:T(8,128)(2,1)S(1)}, bf16[6,16,128]{2,1,0:T(8,128)(2,1)S(1)}, u32[]{:S(2)}, u32[]{:S(2)}) collective-permute-start(bf16[6,16,128]{2,1,0:T(8,128)(2,1)S(1)} %get-tuple-element.25.own_ref), channel_id=1, source_target_pairs={{0,8},{8,0},{16,24},{24,16},{1,9},{9,1},{17,25},{25,17},{2,10},{10... | collective-permute-start | bytes 73736 | tf_op jit(solution)/shard_map/ppermute | solution.py:406
  5.8 5.2 %collective-permute-start.1 = (bf16[2,16,128]{2,1,0:T(8,128)(2,1)S(1)}, bf16[2,16,128]{2,1,0:T(8,128)(2,1)S(1)}, u32[]{:S(2)}, u32[]{:S(2)}) collective-permute-start(bf16[2,16,128]{2,1,0:T(8,128)(2,1)S(1)} %slice.3), channel_id=1, source_target_pairs={{0,16},{8,24},{16,0},{24,8},{1,17},{9,25},{17,1},{25,9},{2,18},{10... | collective-permute-start | bytes 24584 | tf_op jit(solution)/shard_map/ppermute | solution.py:406
  8.4 5.6 %collective-permute-start = (bf16[6,16,128]{2,1,0:T(8,128)(2,1)S(1)}, bf16[6,16,128]{2,1,0:T(8,128)(2,1)S(1)}, u32[]{:S(2)}, u32[]{:S(2)}) collective-permute-start(bf16[6,16,128]{2,1,0:T(8,128)(2,1)S(1)} %get-tuple-element.26), channel_id=1, source_target_pairs={{0,24},{8,16},{16,8},{24,0},{1,25},{9,17},{17,9},{25,1},{2,26},{10... | collective-permute-start | bytes 73736 | tf_op jit(solution)/shard_map/ppermute | solution.py:406
  14.1 11.0 %collective-permute-start.5 = (bf16[44,16,128]{2,1,0:T(8,128)(2,1)S(1)}, bf16[44,16,128]{2,1,0:T(8,128)(2,1)S(1)}, u32[]{:S(2)}, u32[]{:S(2)}) collective-permute-start(bf16[44,16,128]{2,1,0:T(8,128)(2,1)S(1)} %pack.1.after_ref.refs_0_), channel_id=1, source_target_pairs={{0,6},{1,7},{2,4},{3,5},{4,2},{5,3},{6,0},{7,1},{8,14},{9,15},{10,... | collective-permute-start | bytes 540680 | tf_op jit(solution)/shard_map/ppermute | solution.py:406
  16.6 8.5 %collective-permute-start.4 = (bf16[44,16,128]{2,1,0:T(8,128)(2,1)S(1)}, bf16[44,16,128]{2,1,0:T(8,128)(2,1)S(1)}, u32[]{:S(2)}, u32[]{:S(2)}) collective-permute-start(bf16[44,16,128]{2,1,0:T(8,128)(2,1)S(1)} %pack.1.after_ref.refs_0_), channel_id=1, source_target_pairs={{0,4},{1,5},{2,6},{3,7},{4,0},{5,1},{6,2},{7,3},{8,12},{9,13},{10,... | collective-permute-start | bytes 540680 | tf_op jit(solution)/shard_map/ppermute | solution.py:406
  17.1 8.0 %collective-permute-start.3 = (bf16[44,16,128]{2,1,0:T(8,128)(2,1)S(1)}, bf16[44,16,128]{2,1,0:T(8,128)(2,1)S(1)}, u32[]{:S(2)}, u32[]{:S(2)}) collective-permute-start(bf16[44,16,128]{2,1,0:T(8,128)(2,1)S(1)} %pack.1.after_ref.refs_0_), channel_id=1, source_target_pairs={{0,2},{1,3},{2,0},{3,1},{4,6},{5,7},{6,4},{7,5},{8,10},{9,11},{10,... | collective-permute-start | bytes 540680 | tf_op jit(solution)/shard_map/ppermute | solution.py:406
  25.1 2.4 %copy-start = (bf16[32,256,64]{1,2,0:T(8,128)(2,1)S(1)}, bf16[32,256,64]{1,2,0:T(8,128)(2,1)}, u32[]{:S(2)}) copy-start(bf16[32,256,64]{1,2,0:T(8,128)(2,1)} %param.16) | copy-start | bytes 3145732
  25.2 2.3 %collective-permute-start.6 = (bf16[180,16,128]{2,1,0:T(8,128)(2,1)S(1)}, bf16[180,16,128]{2,1,0:T(8,128)(2,1)S(1)}, u32[]{:S(2)}, u32[]{:S(2)}) collective-permute-start(bf16[180,16,128]{2,1,0:T(8,128)(2,1)S(1)} %join.1.a_ref), channel_id=1, source_target_pairs={{0,1},{1,0},{2,3},{3,2},{4,5},{5,4},{6,7},{7,6},{8,9},{9,8},{10,11... | collective-permute-start | bytes 2211848 | tf_op jit(solution)/shard_map/ppermute | solution.py:406
where the time goes:
time: 32.5 us; the launch traced here: 32.3 us
  Pallas kernels  17.7 us (54%)
  starting transfers between devices  9.33 us (29%)
  waiting for transfers between devices  5.21 us (16%)
    ppermute x7, starting transfers between devices, swap(): return lax.ppermute(v, axis, [(i, i ^ k) for i in range(size)])  9.33 us
    pallas_call x1, Pallas kernels, shards(): pl.pallas_call(functools.partial(near_kernel, n0, leaf, cols), out_shape=...  7.46 us
    ppermute x7, waiting for transfers between devices, swap(): return lax.ppermute(v, axis, [(i, i ^ k) for i in range(size)])  5.21 us
    pallas_call x1, Pallas kernels, shards(): pl.pallas_call(functools.partial(product_kernel, n0, leaf, cols, pairs),...  4.82 us
    pallas_call x1, Pallas kernels, shards(): pl.pallas_call(functools.partial(upward_kernel, n0, leaf), out_shape=[blo...  2.7 us
    pallas_call x1, Pallas kernels, shards(): pl.pallas_call(functools.partial(fold_kernel, n0, cols, rows), out_shape=...  2.61 us
  transfers between devices with their start and end apart: 7, of which 2 were waited for; matrix products, arithmetic and copies ran while one was open for 0% of the time, Pallas kernels for 31%

commit v1 on v0

--- a/solution.py
+++ b/solution.py
@@ -10,9 +10,9 @@
 
 SLOTS = 8
 HALO = 2
-STEPS = 8
-CHUNKS = 4
-SENDS = 2
+STEPS = 2
+CHUNKS = 2
+SENDS = 1
 
 
 NT = (((1,), (1,)), ((), ()))
@@ -287,13 +287,13 @@
     for f in lists:
         f.wait()
 
-    @pl.loop(0, n3)
+    @pl.loop(0, n3 // 2)
     def _(t):
         for per, first, spot in (
-            (1, 0, lambda k, i: i3_ref[i, k]),
-            (2, n3, lambda k, i: i2_ref[i, k]),
-            (4, n3 + n2, lambda k, i: i1_ref[k, i]),
-            (8, n3 + n2 + n1, lambda k, i: i0_ref[k, i]),
+            (2, 0, lambda k, i: i3_ref[i, k]),
+            (4, n3, lambda k, i: i2_ref[i, k]),
+            (8, n3 + n2, lambda k, i: i1_ref[k, i]),
+            (16, n3 + n2 + n1, lambda k, i: i0_ref[k, i]),
         ):
             for j in range(per):
                 i = t * per + j
@@ -301,7 +301,7 @@
                     jnp.where(low, table_ref[spot(2 * q, i)], table_ref[spot(2 * q + 1, i)])
                     for q in range(SLOTS // 2)
                 ]
-                blocks = c_ref[first + i] if per < 8 else c0_ref[i]
+                blocks = c_ref[first + i] if first < 7 * n3 else c0_ref[i]
                 field_ref[first + i] = dot(blocks, jnp.concatenate(xs, axis=1), NT)
 
     row, col = lax.axis_index("row"), lax.axis_index("col")

time: 32.5 us -> 30.5 us (0.938)
  Pallas kernels: 17.7 us -> 15.5 us
    pallas_call x1, Pallas kernels: 7.46 us -> 6 us  [shards(): pl.pallas_call(functools.partial(near_kernel, n0, leaf, cols), out_shape=...]
    pallas_call x1, Pallas kernels: 4.82 us -> 4.29 us  [shards(): pl.pallas_call(functools.partial(product_kernel, n0, leaf, cols, pairs),...]
  transfers between devices with their start and end apart: 7 -> 7, of which waited for: 2 -> 2; matrix products, arithmetic and copies ran while one was open for 0% -> 0% of each run, Pallas kernels for 31% -> 28%
where the time goes in v1:
time: 30.5 us; the launch traced here: 30.3 us
  Pallas kernels  15.5 us (51%)
  starting transfers between devices  9.33 us (31%)
  waiting for transfers between devices  5.35 us (18%)
    ppermute x7, starting transfers between devices, swap(): return lax.ppermute(v, axis, [(i, i ^ k) for i in range(size)])  9.33 us
    pallas_call x1, Pallas kernels, shards(): pl.pallas_call(functools.partial(near_kernel, n0, leaf, cols), out_shape=...  6 us
    ppermute x7, waiting for transfers between devices, swap(): return lax.ppermute(v, axis, [(i, i ^ k) for i in range(size)])  5.35 us
    pallas_call x1, Pallas kernels, shards(): pl.pallas_call(functools.partial(product_kernel, n0, leaf, cols, pairs),...  4.29 us
    pallas_call x1, Pallas kernels, shards(): pl.pallas_call(functools.partial(upward_kernel, n0, leaf), out_shape=[blo...  2.7 us
    pallas_call x1, Pallas kernels, shards(): pl.pallas_call(functools.partial(fold_kernel, n0, cols, rows), out_shape=...  2.47 us
  transfers between devices with their start and end apart: 7, of which 2 were waited for; matrix products, arithmetic and copies ran while one was open for 0% of the time, Pallas kernels for 28%

profile of v1, /device:TPU:0, one launch (start us, length us, event | category | flops | bytes accessed | tf_op | source)
XLA Modules:
  0.0 30.3 jit_solution(3060374899799925941)
XLA Ops:
  0.0 2.7 %upward.1 = (bf16[28,16,128]{2,1,0:T(8,128)(2,1)S(1)}, bf16[6,16,128]{2,1,0:T(8,128)(2,1)S(1)}, bf16[6,16,128]{2,1,0:T(8,128)(2,1)S(1)}, bf16[4,16,128]{2,1,0:T(8,128)(2,1)S(1)}, bf16[4,16,128]{2,1,0:T(8,128)(2,1)S(1)}) custom-call(bf16[16,8192]{1,0:T(8,128)(2,1)} %bitcast.13, bf16[16,128,256]{2,1,0:T(8,128)(2,1)} %bitcast.11, ...), custom_call_target="tpu_custom_call" | custom-call | flops 400000000 | bytes 6000000 | tf_op jit(solution)/shard_map/upward/pallas_call | solution.py:392
  2.7 3.1 %collective-permute-start.2 = (bf16[6,16,128]{2,1,0:T(8,128)(2,1)S(1)}, bf16[6,16,128]{2,1,0:T(8,128)(2,1)S(1)}, u32[]{:S(2)}, u32[]{:S(2)}) collective-permute-start(bf16[6,16,128]{2,1,0:T(8,128)(2,1)S(1)} %get-tuple-element.25.own_ref), channel_id=1, source_target_pairs={{0,8},{8,0},{16,24},{24,16},{1,9},{9,1},{17,25},{25,17},{2,10},{10... | collective-permute-start | bytes 73736 | tf_op jit(solution)/shard_map/ppermute | solution.py:406
  5.8 2.6 %collective-permute-start.1 = (bf16[2,16,128]{2,1,0:T(8,128)(2,1)S(1)}, bf16[2,16,128]{2,1,0:T(8,128)(2,1)S(1)}, u32[]{:S(2)}, u32[]{:S(2)}) collective-permute-start(bf16[2,16,128]{2,1,0:T(8,128)(2,1)S(1)} %slice.3), channel_id=1, source_target_pairs={{0,16},{8,24},{16,0},{24,8},{1,17},{9,25},{17,1},{25,9},{2,18},{10... | collective-permute-start | bytes 24584 | tf_op jit(solution)/shard_map/ppermute | solution.py:406
  8.4 0.0 collective-permute-start
  8.4 2.5 %fold.1 = (s32[8,32]{1,0:T(8,128)S(1)}, s32[8,16]{1,0:T(8,128)S(1)}, s32[8,8]{1,0:T(8,128)S(1)}, s32[4,8]{1,0:T(4,128)S(1)}, bf16[28,64,512]{2,1,0:T(8,128)(2,1)S(1)}) custom-call(s32[8,32]{1,0:T(8,128)} %bitcast.24, s32[8,16]{1,0:T(8,128)} %bitcast.25, s32[8,8]{1,0:T(8,128)} %f2_hbm.1, s32[4,8]{1,0:T(4,128)} %f3_hbm.1, bf16[16,8,64,64]{3,2,1,0:T(8,128)(2,1)} %s1_hbm.1, ...), custom_call_target="tpu_custom_call" | custom-call | flops 800000000 | bytes 12000000 | tf_op jit(solution)/shard_map/fold/pallas_call | solution.py:416
  10.9 0.0 collective-permute-done.1.refs_1_
  10.9 3.1 %collective-permute-done.refs_0_ = bf16[6,16,128]{2,1,0:T(8,128)(2,1)S(1)} collective-permute-done((bf16[6,16,128]{2,1,0:T(8,128)(2,1)S(1)}, bf16[6,16,128]{2,1,0:T(8,128)(2,1)S(1)}, u32[]{:S(2)}, u32[]{:S(2)}) %collective-permute-start) | collective-permute-done | bytes 24608 | tf_op jit(solution)/shard_map/ppermute | solution.py:406
  14.0 0.0 collective-permute-done.2.refs_2_
  14.1 2.5 %collective-permute-start.5 = (bf16[44,16,128]{2,1,0:T(8,128)(2,1)S(1)}, bf16[44,16,128]{2,1,0:T(8,128)(2,1)S(1)}, u32[]{:S(2)}, u32[]{:S(2)}) collective-permute-start(bf16[44,16,128]{2,1,0:T(8,128)(2,1)S(1)} %pack.1.after_ref.refs_0_), channel_id=1, source_target_pairs={{0,6},{1,7},{2,4},{3,5},{4,2},{5,3},{6,0},{7,1},{8,14},{9,15},{10,... | collective-permute-start | bytes 540680 | tf_op jit(solution)/shard_map/ppermute | solution.py:406
  16.6 0.5 %collective-permute-start.4 = (bf16[44,16,128]{2,1,0:T(8,128)(2,1)S(1)}, bf16[44,16,128]{2,1,0:T(8,128)(2,1)S(1)}, u32[]{:S(2)}, u32[]{:S(2)}) collective-permute-start(bf16[44,16,128]{2,1,0:T(8,128)(2,1)S(1)} %pack.1.after_ref.refs_0_), channel_id=1, source_target_pairs={{0,4},{1,5},{2,6},{3,7},{4,0},{5,1},{6,2},{7,3},{8,12},{9,13},{10,... | collective-permute-start | bytes 540680 | tf_op jit(solution)/shard_map/ppermute | solution.py:406
  17.1 0.5 %collective-permute-start.3 = (bf16[44,16,128]{2,1,0:T(8,128)(2,1)S(1)}, bf16[44,16,128]{2,1,0:T(8,128)(2,1)S(1)}, u32[]{:S(2)}, u32[]{:S(2)}) collective-permute-start(bf16[44,16,128]{2,1,0:T(8,128)(2,1)S(1)} %pack.1.after_ref.refs_0_), channel_id=1, source_target_pairs={{0,2},{1,3},{2,0},{3,1},{4,6},{5,7},{6,4},{7,5},{8,10},{9,11},{10,... | collective-permute-start | bytes 540680 | tf_op jit(solution)/shard_map/ppermute | solution.py:406
  17.6 6.0 %near.1 = (f32[16,8192]{1,0:T(8,128)S(1)}, bf16[32,64,512]{2,1,0:T(8,128)(2,1)S(1)}) custom-call(s32[2,32]{1,0:T(2,128)} %bitcast.22, bf16[16,8192]{1,0:T(8,128)(2,1)} %bitcast.14, bf16[32,2,256,256]{3,2,1,0:T(8,128)(2,1)} %blocks_hbm.3, bf16[32,8,64,64]{3,2,1,0:T(8,128)(2,1)} %s_hbm.1, bf16[44,16,128]{2,1,0:T(8,128)(2,1)S(1)} %pack.1.after_ref.refs_0_), custom_call_target="tpu_custom_call" | custom-call | flops 1200000000 | bytes 18000000 | tf_op jit(solution)/shard_map/near/pallas_call | solution.py:444
  23.6 0.0 copy-start
  23.7 0.0 collective-permute-done.5.refs_3_
  23.7 0.0 collective-permute-done.4.refs_2_
  23.7 0.0 collective-permute-done.3.refs_1_
  23.7 0.1 join.1.a_ref
  23.7 0.1 collective-permute-start.6
  23.8 2.2 %collective-permute-done.6.b_ref = bf16[180,16,128]{2,1,0:T(8,128)(2,1)S(1)} collective-permute-done((bf16[180,16,128]{2,1,0:T(8,128)(2,1)S(1)}, bf16[180,16,128]{2,1,0:T(8,128)(2,1)S(1)}, u32[]{:S(2)}, u32[]{:S(2)}) %collective-permute-start.6) | collective-permute-done | bytes 737312 | tf_op jit(solution)/shard_map/ppermute | solution.py:406
  26.0 0.0 copy-done
  26.0 4.3 %product.1 = (bf16[16,8192]{1,0:T(8,128)(2,1)}, f32[16,8192]{1,0:T(8,128)S(1)}) custom-call(s32[8,32]{1,0:T(8,128)S(1)} %get-tuple-element.18.i0_hbm, s32[8,16]{1,0:T(8,128)S(1)} %get-tuple-element.19.i1_hbm, s32[8,8]{1,0:T(8,128)S(1)} %get-tuple-element.20.i2_hbm, s32[4,8]{1,0:T(4,128)S(1)} %get-tuple-element.21.after_ref.i3_hbm, ...), custom_call_target="tpu_custom_call", output_to_operand_aliasing={{1}: (13, {})} | custom-call | flops 1000000000 | bytes 15000000 | tf_op jit(solution)/shard_map/product/pallas_call | solution.py:475
  (2 shorter events, 0.0 us)
Async XLA Ops:
  2.7 11.3 %collective-permute-start.2 = (bf16[6,16,128]{2,1,0:T(8,128)(2,1)S(1)}, bf16[6,16,128]{2,1,0:T(8,128)(2,1)S(1)}, u32[]{:S(2)}, u32[]{:S(2)}) collective-permute-start(bf16[6,16,128]{2,1,0:T(8,128)(2,1)S(1)} %get-tuple-element.25.own_ref), channel_id=1, source_target_pairs={{0,8},{8,0},{16,24},{24,16},{1,9},{9,1},{17,25},{25,17},{2,10},{10... | collective-permute-start | bytes 73736 | tf_op jit(solution)/shard_map/ppermute | solution.py:406
  5.8 5.1 %collective-permute-start.1 = (bf16[2,16,128]{2,1,0:T(8,128)(2,1)S(1)}, bf16[2,16,128]{2,1,0:T(8,128)(2,1)S(1)}, u32[]{:S(2)}, u32[]{:S(2)}) collective-permute-start(bf16[2,16,128]{2,1,0:T(8,128)(2,1)S(1)} %slice.3), channel_id=1, source_target_pairs={{0,16},{8,24},{16,0},{24,8},{1,17},{9,25},{17,1},{25,9},{2,18},{10... | collective-permute-start | bytes 24584 | tf_op jit(solution)/shard_map/ppermute | solution.py:406
  8.4 5.6 %collective-permute-start = (bf16[6,16,128]{2,1,0:T(8,128)(2,1)S(1)}, bf16[6,16,128]{2,1,0:T(8,128)(2,1)S(1)}, u32[]{:S(2)}, u32[]{:S(2)}) collective-permute-start(bf16[6,16,128]{2,1,0:T(8,128)(2,1)S(1)} %get-tuple-element.26), channel_id=1, source_target_pairs={{0,24},{8,16},{16,8},{24,0},{1,25},{9,17},{17,9},{25,1},{2,26},{10... | collective-permute-start | bytes 73736 | tf_op jit(solution)/shard_map/ppermute | solution.py:406
  14.1 9.6 %collective-permute-start.5 = (bf16[44,16,128]{2,1,0:T(8,128)(2,1)S(1)}, bf16[44,16,128]{2,1,0:T(8,128)(2,1)S(1)}, u32[]{:S(2)}, u32[]{:S(2)}) collective-permute-start(bf16[44,16,128]{2,1,0:T(8,128)(2,1)S(1)} %pack.1.after_ref.refs_0_), channel_id=1, source_target_pairs={{0,6},{1,7},{2,4},{3,5},{4,2},{5,3},{6,0},{7,1},{8,14},{9,15},{10,... | collective-permute-start | bytes 540680 | tf_op jit(solution)/shard_map/ppermute | solution.py:406
  16.6 7.1 %collective-permute-start.4 = (bf16[44,16,128]{2,1,0:T(8,128)(2,1)S(1)}, bf16[44,16,128]{2,1,0:T(8,128)(2,1)S(1)}, u32[]{:S(2)}, u32[]{:S(2)}) collective-permute-start(bf16[44,16,128]{2,1,0:T(8,128)(2,1)S(1)} %pack.1.after_ref.refs_0_), channel_id=1, source_target_pairs={{0,4},{1,5},{2,6},{3,7},{4,0},{5,1},{6,2},{7,3},{8,12},{9,13},{10,... | collective-permute-start | bytes 540680 | tf_op jit(solution)/shard_map/ppermute | solution.py:406
  17.1 6.6 %collective-permute-start.3 = (bf16[44,16,128]{2,1,0:T(8,128)(2,1)S(1)}, bf16[44,16,128]{2,1,0:T(8,128)(2,1)S(1)}, u32[]{:S(2)}, u32[]{:S(2)}) collective-permute-start(bf16[44,16,128]{2,1,0:T(8,128)(2,1)S(1)} %pack.1.after_ref.refs_0_), channel_id=1, source_target_pairs={{0,2},{1,3},{2,0},{3,1},{4,6},{5,7},{6,4},{7,5},{8,10},{9,11},{10,... | collective-permute-start | bytes 540680 | tf_op jit(solution)/shard_map/ppermute | solution.py:406
  23.6 2.4 %copy-start = (bf16[32,256,64]{1,2,0:T(8,128)(2,1)S(1)}, bf16[32,256,64]{1,2,0:T(8,128)(2,1)}, u32[]{:S(2)}) copy-start(bf16[32,256,64]{1,2,0:T(8,128)(2,1)} %param.16) | copy-start | bytes 3145732
  23.7 2.3 %collective-permute-start.6 = (bf16[180,16,128]{2,1,0:T(8,128)(2,1)S(1)}, bf16[180,16,128]{2,1,0:T(8,128)(2,1)S(1)}, u32[]{:S(2)}, u32[]{:S(2)}) collective-permute-start(bf16[180,16,128]{2,1,0:T(8,128)(2,1)S(1)} %join.1.a_ref), channel_id=1, source_target_pairs={{0,1},{1,0},{2,3},{3,2},{4,5},{5,4},{6,7},{7,6},{8,9},{9,8},{10,11... | collective-permute-start | bytes 2211848 | tf_op jit(solution)/shard_map/ppermute | solution.py:406

commit v2 on v1

--- a/solution.py
+++ b/solution.py
@@ -287,13 +287,13 @@
     for f in lists:
         f.wait()
 
-    @pl.loop(0, n3 // 2)
+    @pl.loop(0, 1)
     def _(t):
         for per, first, spot in (
-            (2, 0, lambda k, i: i3_ref[i, k]),
-            (4, n3, lambda k, i: i2_ref[i, k]),
-            (8, n3 + n2, lambda k, i: i1_ref[k, i]),
-            (16, n3 + n2 + n1, lambda k, i: i0_ref[k, i]),
+            (n3, 0, lambda k, i: i3_ref[i, k]),
+            (n2, n3, lambda k, i: i2_ref[i, k]),
+            (n1, n3 + n2, lambda k, i: i1_ref[k, i]),
+            (n0, n3 + n2 + n1, lambda k, i: i0_ref[k, i]),
         ):
             for j in range(per):
                 i = t * per + j

time: 30.5 us -> 30.3 us (level)
  no operation moved by 1% of the time
where the time goes in v2:
time: 30.3 us; the launch traced here: 30.2 us
  Pallas kernels  15.4 us (51%)
  starting transfers between devices  9.33 us (31%)
  waiting for transfers between devices  5.35 us (18%)
    ppermute x7, starting transfers between devices, swap(): return lax.ppermute(v, axis, [(i, i ^ k) for i in range(size)])  9.33 us
    pallas_call x1, Pallas kernels, shards(): pl.pallas_call(functools.partial(near_kernel, n0, leaf, cols), out_shape=...  6 us
    ppermute x7, waiting for transfers between devices, swap(): return lax.ppermute(v, axis, [(i, i ^ k) for i in range(size)])  5.35 us
    pallas_call x1, Pallas kernels, shards(): pl.pallas_call(functools.partial(product_kernel, n0, leaf, cols, pairs),...  4.14 us
    pallas_call x1, Pallas kernels, shards(): pl.pallas_call(functools.partial(upward_kernel, n0, leaf), out_shape=[blo...  2.7 us
    pallas_call x1, Pallas kernels, shards(): pl.pallas_call(functools.partial(fold_kernel, n0, cols, rows), out_shape=...  2.47 us
  transfers between devices with their start and end apart: 7, of which 2 were waited for; matrix products, arithmetic and copies ran while one was open for 0% of the time, Pallas kernels for 28%

profile of v2, /device:TPU:0, one launch (start us, length us, event | category | flops | bytes accessed | tf_op | source)
XLA Modules:
  0.0 30.2 jit_solution(15255108375418572123)
XLA Ops:
  0.0 2.7 %upward.1 = (bf16[28,16,128]{2,1,0:T(8,128)(2,1)S(1)}, bf16[6,16,128]{2,1,0:T(8,128)(2,1)S(1)}, bf16[6,16,128]{2,1,0:T(8,128)(2,1)S(1)}, bf16[4,16,128]{2,1,0:T(8,128)(2,1)S(1)}, bf16[4,16,128]{2,1,0:T(8,128)(2,1)S(1)}) custom-call(bf16[16,8192]{1,0:T(8,128)(2,1)} %bitcast.13, bf16[16,128,256]{2,1,0:T(8,128)(2,1)} %bitcast.11, ...), custom_call_target="tpu_custom_call" | custom-call | flops 400000000 | bytes 6000000 | tf_op jit(solution)/shard_map/upward/pallas_call | solution.py:392
  2.7 3.1 %collective-permute-start.2 = (bf16[6,16,128]{2,1,0:T(8,128)(2,1)S(1)}, bf16[6,16,128]{2,1,0:T(8,128)(2,1)S(1)}, u32[]{:S(2)}, u32[]{:S(2)}) collective-permute-start(bf16[6,16,128]{2,1,0:T(8,128)(2,1)S(1)} %get-tuple-element.25.own_ref), channel_id=1, source_target_pairs={{0,8},{8,0},{16,24},{24,16},{1,9},{9,1},{17,25},{25,17},{2,10},{10... | collective-permute-start | bytes 73736 | tf_op jit(solution)/shard_map/ppermute | solution.py:406
  5.8 2.6 %collective-permute-start.1 = (bf16[2,16,128]{2,1,0:T(8,128)(2,1)S(1)}, bf16[2,16,128]{2,1,0:T(8,128)(2,1)S(1)}, u32[]{:S(2)}, u32[]{:S(2)}) collective-permute-start(bf16[2,16,128]{2,1,0:T(8,128)(2,1)S(1)} %slice.3), channel_id=1, source_target_pairs={{0,16},{8,24},{16,0},{24,8},{1,17},{9,25},{17,1},{25,9},{2,18},{10... | collective-permute-start | bytes 24584 | tf_op jit(solution)/shard_map/ppermute | solution.py:406
  8.4 0.0 collective-permute-start
  8.4 2.5 %fold.1 = (s32[8,32]{1,0:T(8,128)S(1)}, s32[8,16]{1,0:T(8,128)S(1)}, s32[8,8]{1,0:T(8,128)S(1)}, s32[4,8]{1,0:T(4,128)S(1)}, bf16[28,64,512]{2,1,0:T(8,128)(2,1)S(1)}) custom-call(s32[8,32]{1,0:T(8,128)} %bitcast.24, s32[8,16]{1,0:T(8,128)} %bitcast.25, s32[8,8]{1,0:T(8,128)} %f2_hbm.1, s32[4,8]{1,0:T(4,128)} %f3_hbm.1, bf16[16,8,64,64]{3,2,1,0:T(8,128)(2,1)} %s1_hbm.1, ...), custom_call_target="tpu_custom_call" | custom-call | flops 800000000 | bytes 12000000 | tf_op jit(solution)/shard_map/fold/pallas_call | solution.py:416
  10.9 0.0 collective-permute-done.1.refs_1_
  10.9 3.1 %collective-permute-done.refs_0_ = bf16[6,16,128]{2,1,0:T(8,128)(2,1)S(1)} collective-permute-done((bf16[6,16,128]{2,1,0:T(8,128)(2,1)S(1)}, bf16[6,16,128]{2,1,0:T(8,128)(2,1)S(1)}, u32[]{:S(2)}, u32[]{:S(2)}) %collective-permute-start) | collective-permute-done | bytes 24608 | tf_op jit(solution)/shard_map/ppermute | solution.py:406
  14.0 0.0 collective-permute-done.2.refs_2_
  14.1 2.5 %collective-permute-start.5 = (bf16[44,16,128]{2,1,0:T(8,128)(2,1)S(1)}, bf16[44,16,128]{2,1,0:T(8,128)(2,1)S(1)}, u32[]{:S(2)}, u32[]{:S(2)}) collective-permute-start(bf16[44,16,128]{2,1,0:T(8,128)(2,1)S(1)} %pack.1.after_ref.refs_0_), channel_id=1, source_target_pairs={{0,6},{1,7},{2,4},{3,5},{4,2},{5,3},{6,0},{7,1},{8,14},{9,15},{10,... | collective-permute-start | bytes 540680 | tf_op jit(solution)/shard_map/ppermute | solution.py:406
  16.6 0.5 %collective-permute-start.4 = (bf16[44,16,128]{2,1,0:T(8,128)(2,1)S(1)}, bf16[44,16,128]{2,1,0:T(8,128)(2,1)S(1)}, u32[]{:S(2)}, u32[]{:S(2)}) collective-permute-start(bf16[44,16,128]{2,1,0:T(8,128)(2,1)S(1)} %pack.1.after_ref.refs_0_), channel_id=1, source_target_pairs={{0,4},{1,5},{2,6},{3,7},{4,0},{5,1},{6,2},{7,3},{8,12},{9,13},{10,... | collective-permute-start | bytes 540680 | tf_op jit(solution)/shard_map/ppermute | solution.py:406
  17.1 0.5 %collective-permute-start.3 = (bf16[44,16,128]{2,1,0:T(8,128)(2,1)S(1)}, bf16[44,16,128]{2,1,0:T(8,128)(2,1)S(1)}, u32[]{:S(2)}, u32[]{:S(2)}) collective-permute-start(bf16[44,16,128]{2,1,0:T(8,128)(2,1)S(1)} %pack.1.after_ref.refs_0_), channel_id=1, source_target_pairs={{0,2},{1,3},{2,0},{3,1},{4,6},{5,7},{6,4},{7,5},{8,10},{9,11},{10,... | collective-permute-start | bytes 540680 | tf_op jit(solution)/shard_map/ppermute | solution.py:406
  17.6 6.0 %near.1 = (f32[16,8192]{1,0:T(8,128)S(1)}, bf16[32,64,512]{2,1,0:T(8,128)(2,1)S(1)}) custom-call(s32[2,32]{1,0:T(2,128)} %bitcast.22, bf16[16,8192]{1,0:T(8,128)(2,1)} %bitcast.14, bf16[32,2,256,256]{3,2,1,0:T(8,128)(2,1)} %blocks_hbm.3, bf16[32,8,64,64]{3,2,1,0:T(8,128)(2,1)} %s_hbm.1, bf16[44,16,128]{2,1,0:T(8,128)(2,1)S(1)} %pack.1.after_ref.refs_0_), custom_call_target="tpu_custom_call" | custom-call | flops 1200000000 | bytes 18000000 | tf_op jit(solution)/shard_map/near/pallas_call | solution.py:444
  23.6 0.0 copy-start
  23.7 0.0 collective-permute-done.5.refs_3_
  23.7 0.0 collective-permute-done.4.refs_2_
  23.7 0.0 collective-permute-done.3.refs_1_
  23.7 0.1 join.1.a_ref
  23.7 0.1 collective-permute-start.6
  23.8 2.2 %collective-permute-done.6.b_ref = bf16[180,16,128]{2,1,0:T(8,128)(2,1)S(1)} collective-permute-done((bf16[180,16,128]{2,1,0:T(8,128)(2,1)S(1)}, bf16[180,16,128]{2,1,0:T(8,128)(2,1)S(1)}, u32[]{:S(2)}, u32[]{:S(2)}) %collective-permute-start.6) | collective-permute-done | bytes 737312 | tf_op jit(solution)/shard_map/ppermute | solution.py:406
  26.0 0.0 copy-done
  26.0 4.1 %product.1 = (bf16[16,8192]{1,0:T(8,128)(2,1)}, f32[16,8192]{1,0:T(8,128)S(1)}) custom-call(s32[8,32]{1,0:T(8,128)S(1)} %get-tuple-element.18.i0_hbm, s32[8,16]{1,0:T(8,128)S(1)} %get-tuple-element.19.i1_hbm, s32[8,8]{1,0:T(8,128)S(1)} %get-tuple-element.20.i2_hbm, s32[4,8]{1,0:T(4,128)S(1)} %get-tuple-element.21.after_ref.i3_hbm, ...), custom_call_target="tpu_custom_call", output_to_operand_aliasing={{1}: (13, {})} | custom-call | flops 1000000000 | bytes 15000000 | tf_op jit(solution)/shard_map/product/pallas_call | solution.py:475
  (2 shorter events, 0.0 us)
Async XLA Ops:
  2.7 11.3 %collective-permute-start.2 = (bf16[6,16,128]{2,1,0:T(8,128)(2,1)S(1)}, bf16[6,16,128]{2,1,0:T(8,128)(2,1)S(1)}, u32[]{:S(2)}, u32[]{:S(2)}) collective-permute-start(bf16[6,16,128]{2,1,0:T(8,128)(2,1)S(1)} %get-tuple-element.25.own_ref), channel_id=1, source_target_pairs={{0,8},{8,0},{16,24},{24,16},{1,9},{9,1},{17,25},{25,17},{2,10},{10... | collective-permute-start | bytes 73736 | tf_op jit(solution)/shard_map/ppermute | solution.py:406
  5.8 5.1 %collective-permute-start.1 = (bf16[2,16,128]{2,1,0:T(8,128)(2,1)S(1)}, bf16[2,16,128]{2,1,0:T(8,128)(2,1)S(1)}, u32[]{:S(2)}, u32[]{:S(2)}) collective-permute-start(bf16[2,16,128]{2,1,0:T(8,128)(2,1)S(1)} %slice.3), channel_id=1, source_target_pairs={{0,16},{8,24},{16,0},{24,8},{1,17},{9,25},{17,1},{25,9},{2,18},{10... | collective-permute-start | bytes 24584 | tf_op jit(solution)/shard_map/ppermute | solution.py:406
  8.4 5.6 %collective-permute-start = (bf16[6,16,128]{2,1,0:T(8,128)(2,1)S(1)}, bf16[6,16,128]{2,1,0:T(8,128)(2,1)S(1)}, u32[]{:S(2)}, u32[]{:S(2)}) collective-permute-start(bf16[6,16,128]{2,1,0:T(8,128)(2,1)S(1)} %get-tuple-element.26), channel_id=1, source_target_pairs={{0,24},{8,16},{16,8},{24,0},{1,25},{9,17},{17,9},{25,1},{2,26},{10... | collective-permute-start | bytes 73736 | tf_op jit(solution)/shard_map/ppermute | solution.py:406
  14.1 9.6 %collective-permute-start.5 = (bf16[44,16,128]{2,1,0:T(8,128)(2,1)S(1)}, bf16[44,16,128]{2,1,0:T(8,128)(2,1)S(1)}, u32[]{:S(2)}, u32[]{:S(2)}) collective-permute-start(bf16[44,16,128]{2,1,0:T(8,128)(2,1)S(1)} %pack.1.after_ref.refs_0_), channel_id=1, source_target_pairs={{0,6},{1,7},{2,4},{3,5},{4,2},{5,3},{6,0},{7,1},{8,14},{9,15},{10,... | collective-permute-start | bytes 540680 | tf_op jit(solution)/shard_map/ppermute | solution.py:406
  16.6 7.1 %collective-permute-start.4 = (bf16[44,16,128]{2,1,0:T(8,128)(2,1)S(1)}, bf16[44,16,128]{2,1,0:T(8,128)(2,1)S(1)}, u32[]{:S(2)}, u32[]{:S(2)}) collective-permute-start(bf16[44,16,128]{2,1,0:T(8,128)(2,1)S(1)} %pack.1.after_ref.refs_0_), channel_id=1, source_target_pairs={{0,4},{1,5},{2,6},{3,7},{4,0},{5,1},{6,2},{7,3},{8,12},{9,13},{10,... | collective-permute-start | bytes 540680 | tf_op jit(solution)/shard_map/ppermute | solution.py:406
  17.1 6.6 %collective-permute-start.3 = (bf16[44,16,128]{2,1,0:T(8,128)(2,1)S(1)}, bf16[44,16,128]{2,1,0:T(8,128)(2,1)S(1)}, u32[]{:S(2)}, u32[]{:S(2)}) collective-permute-start(bf16[44,16,128]{2,1,0:T(8,128)(2,1)S(1)} %pack.1.after_ref.refs_0_), channel_id=1, source_target_pairs={{0,2},{1,3},{2,0},{3,1},{4,6},{5,7},{6,4},{7,5},{8,10},{9,11},{10,... | collective-permute-start | bytes 540680 | tf_op jit(solution)/shard_map/ppermute | solution.py:406
  23.6 2.4 %copy-start = (bf16[32,256,64]{1,2,0:T(8,128)(2,1)S(1)}, bf16[32,256,64]{1,2,0:T(8,128)(2,1)}, u32[]{:S(2)}) copy-start(bf16[32,256,64]{1,2,0:T(8,128)(2,1)} %param.16) | copy-start | bytes 3145732
  23.7 2.3 %collective-permute-start.6 = (bf16[180,16,128]{2,1,0:T(8,128)(2,1)S(1)}, bf16[180,16,128]{2,1,0:T(8,128)(2,1)S(1)}, u32[]{:S(2)}, u32[]{:S(2)}) collective-permute-start(bf16[180,16,128]{2,1,0:T(8,128)(2,1)S(1)} %join.1.a_ref), channel_id=1, source_target_pairs={{0,1},{1,0},{2,3},{3,2},{4,5},{5,4},{6,7},{7,6},{8,9},{9,8},{10,11... | collective-permute-start | bytes 2211848 | tf_op jit(solution)/shard_map/ppermute | solution.py:406
